TPU v7x, 32 devices: a whole 2x2x4 slice. The times are simulated.
32 devices in a mesh: terms: 32 (over z, y, x, core).
Axes of the slice: x: 2, y: 2, z: 4, core: 2. Of those that a mesh axis runs over, the one named last changes fastest.
Arguments:
- psi: float32 [2, 256, 4, 4, 256], replicated
- left_env: bfloat16 [256, 256, 256], P('terms')
- phys_op: bfloat16 [256, 16, 16], P('terms')
- right_env: bfloat16 [256, 256, 256], P('terms')
Outputs:
- output 1: float32 [2, 7, 256, 4, 4, 256], P(None, None, 'terms')
- output 2: float32 [2, 6], replicated
- output 3: float32 [2, 6], replicated
All inputs are finite; a program needn't handle non-finite values.
Results may differ from a plain program's by a relative error of at most 0.0122832.
Values are sent between devices in bfloat16 or wider.
A program may use at most 1 GiB of HBM per device.

v0:
```python
import jax
import jax.numpy as jnp
from jax import lax
from jax.sharding import PartitionSpec as P

LANCZOS_STEPS = 6


def solution(mesh):
    dev_count = mesh.shape['terms']

    def device_fn(psi, left_loc, phys_loc, right_loc):
        roots, bond_dim, phys_dim = psi.shape[0], psi.shape[1], psi.shape[2]
        pairs = phys_dim * phys_dim
        rows = bond_dim // dev_count
        n_elems = bond_dim * pairs * bond_dim
        psi_mat = psi.reshape(roots, bond_dim, pairs, bond_dim)
        norms = jnp.sqrt(jnp.sum(psi_mat * psi_mat, axis=(1, 2, 3)) / n_elems)
        v_full = psi_mat / norms[:, None, None, None]
        row_start = lax.axis_index('terms') * rows
        v_cur = lax.dynamic_slice_in_dim(v_full, row_start, rows, axis=1)
        v_in = v_full.astype(jnp.bfloat16)
        v_prev = jnp.zeros_like(v_cur)
        beta_prev = jnp.zeros((roots,), jnp.float32)
        vectors = [v_cur]
        alphas = []
        betas = []
        for step_idx in range(LANCZOS_STEPS):
            right_part = jnp.einsum('rcup,kbp->krcub', v_in, right_loc, preferred_element_type=jnp.float32).astype(jnp.bfloat16)
            mid_part = jnp.einsum('kqu,krcub->krcqb', phys_loc, right_part, preferred_element_type=jnp.float32).astype(jnp.bfloat16)
            part_sigma = jnp.einsum('kac,krcqb->raqb', left_loc, mid_part, preferred_element_type=jnp.float32)
            sigma = lax.psum_scatter(part_sigma, 'terms', scatter_dimension=1, tiled=True)
            alpha = lax.psum(jnp.sum(sigma * v_cur, axis=(1, 2, 3)), 'terms') / n_elems
            residual = sigma - alpha[:, None, None, None] * v_cur - beta_prev[:, None, None, None] * v_prev
            beta = jnp.sqrt(lax.psum(jnp.sum(residual * residual, axis=(1, 2, 3)), 'terms') / n_elems)
            v_next = residual / beta[:, None, None, None]
            if step_idx + 1 < LANCZOS_STEPS:
                v_in = lax.all_gather(v_next.astype(jnp.bfloat16), 'terms', axis=1, tiled=True)
            vectors.append(v_next)
            alphas.append(alpha)
            betas.append(beta)
            v_prev, v_cur, beta_prev = v_cur, v_next, beta
        stacked = jnp.stack(vectors, axis=1).reshape(roots, LANCZOS_STEPS + 1, rows, phys_dim, phys_dim, bond_dim)
        return stacked, jnp.stack(alphas, axis=1), jnp.stack(betas, axis=1)

    return jax.shard_map(device_fn, mesh=mesh, in_specs=(P(), P('terms'), P('terms'), P('terms')), out_specs=(P(None, None, 'terms'), P(), P()), check_vma=False)
```

profile of v0, /device:TPU:0, one launch (start us, length us, event | category | flops | bytes accessed | tf_op | source)
XLA Modules:
  0.0 2312.9 jit_solution(12083985777171693217)
XLA Ops:
  42.7 33.1 %convert_bitcast_fusion.10 = bf16[8,2,256,16,256]{4,3,2,1,0:T(8,128)(2,1)} fusion(bf16[8,2,256,16,256]{4,2,0,3,1:T(8,128)(2,1)} %convert_bitcast_fusion.11, bf16[8,16,16]{2,1,0:T(8,128)(2,1)S(1)} %copy-done.5), kind=kOutput, calls=%fused_computation.34 | convolution fusion | flops 553648128 | bytes 67112960 | tf_op jit(solution)/shard_map/kqu,krcub->krcqb/dot_general | solution.py:30
  115.9 151.5 %reduce-scatter.7.cloned.1.call-done = f32[2,8,16,256]{3,2,0,1:T(8,128)} async-done(((f32[2,256,16,256]{3,2,0,1:T(8,128)}), f32[2,8,16,256]{3,2,0,1:T(8,128)}) %reduce-scatter.7.cloned.1.call-update) | async-done | bytes 262160 | tf_op jit(solution)/shard_map/reduce_scatter | solution.py:32
  268.7 37.0 %psum.84 = f32[2]{0:T(128)S(1)} all-reduce(f32[2]{0:T(128)S(1)} %get-tuple-element.32), channel_id=1, replica_groups=mesh['terms'=32] {'terms'}, use_global_device_ids=true, to_apply=%region_3.0 | all-reduce | flops 2 | bytes 16 | tf_op jit(solution)/shard_map/psum | solution.py:33
  307.4 40.9 %psum.85 = f32[2]{0:T(128)S(1)} all-reduce(f32[2]{0:T(128)S(1)} %multiply_reduce_fusion.11), channel_id=1, replica_groups=mesh['terms'=32] {'terms'}, use_global_device_ids=true, to_apply=%region_5.0 | all-reduce | flops 2 | bytes 16 | tf_op jit(solution)/shard_map/psum | solution.py:35
  350.8 62.5 %all-gather.6.cloned.1.call-done = bf16[2,256,16,256]{3,2,0,1:T(8,128)(2,1)} async-done(((bf16[2,8,16,256]{3,2,0,1:T(8,128)(2,1)}), bf16[2,256,16,256]{3,2,0,1:T(8,128)(2,1)}) %all-gather.6.cloned.1.call-update) | async-done | bytes 4194320 | tf_op jit(solution)/shard_map/all_gather | solution.py:38
  439.1 33.0 %convert_bitcast_fusion.8 = bf16[8,2,256,16,256]{4,3,2,1,0:T(8,128)(2,1)} fusion(bf16[8,2,256,16,256]{4,2,0,3,1:T(8,128)(2,1)} %convert_bitcast_fusion.9, bf16[8,16,16]{2,1,0:T(8,128)(2,1)S(1)} %copy-done.5), kind=kOutput, calls=%fused_computation.32 | convolution fusion | flops 553648128 | bytes 67112960 | tf_op jit(solution)/shard_map/kqu,krcub->krcqb/dot_general | solution.py:30
  512.4 146.8 %reduce-scatter.9.cloned.1.call-done = f32[2,8,16,256]{3,2,0,1:T(8,128)} async-done(((f32[2,256,16,256]{3,2,0,1:T(8,128)}), f32[2,8,16,256]{3,2,0,1:T(8,128)}) %reduce-scatter.9.cloned.1.call-update) | async-done | bytes 262160 | tf_op jit(solution)/shard_map/reduce_scatter | solution.py:32
  660.3 37.0 %psum.86 = f32[2]{0:T(128)S(1)} all-reduce(f32[2]{0:T(128)S(1)} %multiply_reduce_fusion.10), channel_id=1, replica_groups=mesh['terms'=32] {'terms'}, use_global_device_ids=true, to_apply=%region_8.0 | all-reduce | flops 2 | bytes 16 | tf_op jit(solution)/shard_map/psum | solution.py:33
  699.0 40.9 %psum.87 = f32[2]{0:T(128)S(1)} all-reduce(f32[2]{0:T(128)S(1)} %get-tuple-element.28), channel_id=1, replica_groups=mesh['terms'=32] {'terms'}, use_global_device_ids=true, to_apply=%region_10.0 | all-reduce | flops 2 | bytes 16 | tf_op jit(solution)/shard_map/psum | solution.py:35
  741.4 62.5 %all-gather.8.cloned.1.call-done = bf16[2,256,16,256]{3,2,0,1:T(8,128)(2,1)} async-done(((bf16[2,8,16,256]{3,2,0,1:T(8,128)(2,1)}), bf16[2,256,16,256]{3,2,0,1:T(8,128)(2,1)}) %all-gather.8.cloned.1.call-update) | async-done | bytes 4194320 | tf_op jit(solution)/shard_map/all_gather | solution.py:38
  829.7 33.0 %convert_bitcast_fusion.6 = bf16[8,2,256,16,256]{4,3,2,1,0:T(8,128)(2,1)} fusion(bf16[8,2,256,16,256]{4,2,0,3,1:T(8,128)(2,1)} %convert_bitcast_fusion.7, bf16[8,16,16]{2,1,0:T(8,128)(2,1)S(1)} %copy-done.5), kind=kOutput, calls=%fused_computation.30 | convolution fusion | flops 553648128 | bytes 67112960 | tf_op jit(solution)/shard_map/kqu,krcub->krcqb/dot_general | solution.py:30
  862.7 29.9 %fusion.49 = f32[2,256,16,256]{1,3,2,0:T(8,128)} fusion(bf16[8,2,256,16,256]{4,3,2,1,0:T(8,128)(2,1)} %convert_bitcast_fusion.6, bf16[8,256,256]{2,1,0:T(8,128)(2,1)} %param.5), kind=kOutput, calls=%fused_computation.47 | convolution fusion | flops 8589934592 | bytes 42991616 | tf_op jit(solution)/shard_map/kac,krcqb->raqb/dot_general | solution.py:31
  903.0 146.8 %reduce-scatter.11.cloned.1.call-done = f32[2,8,16,256]{3,2,0,1:T(8,128)} async-done(((f32[2,256,16,256]{3,2,0,1:T(8,128)}), f32[2,8,16,256]{3,2,0,1:T(8,128)}) %reduce-scatter.11.cloned.1.call-update) | async-done | bytes 262160 | tf_op jit(solution)/shard_map/reduce_scatter | solution.py:32
  1050.9 37.0 %psum.88 = f32[2]{0:T(128)S(1)} all-reduce(f32[2]{0:T(128)S(1)} %multiply_reduce_fusion.8), channel_id=1, replica_groups=mesh['terms'=32] {'terms'}, use_global_device_ids=true, to_apply=%region_13.0 | all-reduce | flops 2 | bytes 16 | tf_op jit(solution)/shard_map/psum | solution.py:33
  1089.7 40.9 %psum.89 = f32[2]{0:T(128)S(1)} all-reduce(f32[2]{0:T(128)S(1)} %get-tuple-element.24), channel_id=1, replica_groups=mesh['terms'=32] {'terms'}, use_global_device_ids=true, to_apply=%region_15.0 | all-reduce | flops 2 | bytes 16 | tf_op jit(solution)/shard_map/psum | solution.py:35
  1132.0 62.5 %all-gather.10.cloned.1.call-done = bf16[2,256,16,256]{3,2,0,1:T(8,128)(2,1)} async-done(((bf16[2,8,16,256]{3,2,0,1:T(8,128)(2,1)}), bf16[2,256,16,256]{3,2,0,1:T(8,128)(2,1)}) %all-gather.10.cloned.1.call-update) | async-done | bytes 4194320 | tf_op jit(solution)/shard_map/all_gather | solution.py:38
  1220.3 33.0 %convert_bitcast_fusion.4 = bf16[8,2,256,16,256]{4,3,2,1,0:T(8,128)(2,1)} fusion(bf16[8,2,256,16,256]{4,2,0,3,1:T(8,128)(2,1)} %convert_bitcast_fusion.5, bf16[8,16,16]{2,1,0:T(8,128)(2,1)S(1)} %copy-done.5), kind=kOutput, calls=%fused_computation.28 | convolution fusion | flops 553648128 | bytes 67112960 | tf_op jit(solution)/shard_map/kqu,krcub->krcqb/dot_general | solution.py:30
  1253.3 29.9 %fusion.52 = f32[2,256,16,256]{1,3,2,0:T(8,128)} fusion(bf16[8,2,256,16,256]{4,3,2,1,0:T(8,128)(2,1)} %convert_bitcast_fusion.4, bf16[8,256,256]{2,1,0:T(8,128)(2,1)} %param.5), kind=kOutput, calls=%fused_computation.48 | convolution fusion | flops 8589934592 | bytes 42991616 | tf_op jit(solution)/shard_map/kac,krcqb->raqb/dot_general | solution.py:31
  1293.6 147.2 %reduce-scatter.13.cloned.1.call-done = f32[2,8,16,256]{3,2,0,1:T(8,128)} async-done(((f32[2,256,16,256]{3,2,0,1:T(8,128)}), f32[2,8,16,256]{3,2,0,1:T(8,128)}) %reduce-scatter.13.cloned.1.call-update) | async-done | bytes 262160 | tf_op jit(solution)/shard_map/reduce_scatter | solution.py:32
  1442.0 37.0 %psum.90 = f32[2]{0:T(128)S(1)} all-reduce(f32[2]{0:T(128)S(1)} %multiply_reduce_fusion.6), channel_id=1, replica_groups=mesh['terms'=32] {'terms'}, use_global_device_ids=true, to_apply=%region_18.0 | all-reduce | flops 2 | bytes 16 | tf_op jit(solution)/shard_map/psum | solution.py:33
  1480.2 40.9 %psum.91 = f32[2]{0:T(128)S(1)} all-reduce(f32[2]{0:T(128)S(1)} %get-tuple-element.20), channel_id=1, replica_groups=mesh['terms'=32] {'terms'}, use_global_device_ids=true, to_apply=%region_20.0 | all-reduce | flops 2 | bytes 16 | tf_op jit(solution)/shard_map/psum | solution.py:35
  1522.0 62.5 %all-gather.12.cloned.1.call-done = bf16[2,256,16,256]{3,2,0,1:T(8,128)(2,1)} async-done(((bf16[2,8,16,256]{3,2,0,1:T(8,128)(2,1)}), bf16[2,256,16,256]{3,2,0,1:T(8,128)(2,1)}) %all-gather.12.cloned.1.call-update) | async-done | bytes 4194320 | tf_op jit(solution)/shard_map/all_gather | solution.py:38
  1610.2 33.0 %convert_bitcast_fusion.2 = bf16[8,2,256,16,256]{4,3,2,1,0:T(8,128)(2,1)} fusion(bf16[8,2,256,16,256]{4,2,0,3,1:T(8,128)(2,1)} %convert_bitcast_fusion.3, bf16[8,16,16]{2,1,0:T(8,128)(2,1)S(1)} %copy-done.5), kind=kOutput, calls=%fused_computation.26 | convolution fusion | flops 553648128 | bytes 67112960 | tf_op jit(solution)/shard_map/kqu,krcub->krcqb/dot_general | solution.py:30
  1643.2 29.9 %fusion.55 = f32[2,256,16,256]{1,3,2,0:T(8,128)} fusion(bf16[8,2,256,16,256]{4,3,2,1,0:T(8,128)(2,1)} %convert_bitcast_fusion.2, bf16[8,256,256]{2,1,0:T(8,128)(2,1)} %param.5), kind=kOutput, calls=%fused_computation.49 | convolution fusion | flops 8589934592 | bytes 42991616 | tf_op jit(solution)/shard_map/kac,krcqb->raqb/dot_general | solution.py:31
  1683.6 146.8 %reduce-scatter.15.cloned.1.call-done = f32[2,8,16,256]{3,2,0,1:T(8,128)} async-done(((f32[2,256,16,256]{3,2,0,1:T(8,128)}), f32[2,8,16,256]{3,2,0,1:T(8,128)}) %reduce-scatter.15.cloned.1.call-update) | async-done | bytes 262160 | tf_op jit(solution)/shard_map/reduce_scatter | solution.py:32
  1831.5 37.0 %psum.92 = f32[2]{0:T(128)S(1)} all-reduce(f32[2]{0:T(128)S(1)} %multiply_reduce_fusion.4), channel_id=1, replica_groups=mesh['terms'=32] {'terms'}, use_global_device_ids=true, to_apply=%region_23.0 | all-reduce | flops 2 | bytes 16 | tf_op jit(solution)/shard_map/psum | solution.py:33
  1869.7 40.9 %psum.93 = f32[2]{0:T(128)S(1)} all-reduce(f32[2]{0:T(128)S(1)} %get-tuple-element.16), channel_id=1, replica_groups=mesh['terms'=32] {'terms'}, use_global_device_ids=true, to_apply=%region_25.0 | all-reduce | flops 2 | bytes 16 | tf_op jit(solution)/shard_map/psum | solution.py:35
  1911.5 62.5 %all-gather.14.cloned.1.call-done = bf16[2,256,16,256]{3,2,0,1:T(8,128)(2,1)} async-done(((bf16[2,8,16,256]{3,2,0,1:T(8,128)(2,1)}), bf16[2,256,16,256]{3,2,0,1:T(8,128)(2,1)}) %all-gather.14.cloned.1.call-update) | async-done | bytes 4194320 | tf_op jit(solution)/shard_map/all_gather | solution.py:38
  1999.8 33.0 %convert_bitcast_fusion = bf16[8,2,256,16,256]{4,3,2,1,0:T(8,128)(2,1)} fusion(bf16[8,2,256,16,256]{4,2,0,3,1:T(8,128)(2,1)} %convert_bitcast_fusion.1, bf16[8,16,16]{2,1,0:T(8,128)(2,1)S(1)} %copy-done.5), kind=kOutput, calls=%fused_computation.24 | convolution fusion | flops 553648128 | bytes 67112960 | tf_op jit(solution)/shard_map/kqu,krcub->krcqb/dot_general | solution.py:30
  2078.2 141.5 %reduce-scatter.17.cloned.1.call-done = f32[2,8,16,256]{3,2,0,1:T(8,128)} async-done(((f32[2,256,16,256]{3,2,0,1:T(8,128)}), f32[2,8,16,256]{3,2,0,1:T(8,128)}) %reduce-scatter.17.cloned.1.call-update) | async-done | bytes 262160 | tf_op jit(solution)/shard_map/reduce_scatter | solution.py:32
  2221.0 37.0 %psum.94 = f32[2]{0:T(128)S(1)} all-reduce(f32[2]{0:T(128)S(1)} %multiply_reduce_fusion.2), channel_id=1, replica_groups=mesh['terms'=32] {'terms'}, use_global_device_ids=true, to_apply=%region_28.0 | all-reduce | flops 2 | bytes 16 | tf_op jit(solution)/shard_map/psum | solution.py:33
  2259.3 40.9 %psum.95 = f32[2]{0:T(128)S(1)} all-reduce(f32[2]{0:T(128)S(1)} %get-tuple-element.12), channel_id=1, replica_groups=mesh['terms'=32] {'terms'}, use_global_device_ids=true, to_apply=%region_30.0 | all-reduce | flops 2 | bytes 16 | tf_op jit(solution)/shard_map/psum | solution.py:35
  (124 shorter events, 350.2 us)
Async XLA Ops:
  7.2 18.3 copy-start
  7.2 260.3 %reduce-scatter.7.cloned.1.call-start = ((), (), s32[]{:S(2)}) async-start(), calls=%async_computation.6 | async-start | bytes 8650752 | tf_op jit(solution)/shard_map/reduce_scatter | solution.py:32
  15.5 27.2 %copy-start.5 = (bf16[8,16,16]{2,1,0:T(8,128)(2,1)S(1)}, bf16[8,16,16]{2,1,0:T(8,128)(2,1)}, u32[]{:S(2)}) copy-start(bf16[8,16,16]{2,1,0:T(8,128)(2,1)} %param.6) | copy-start | bytes 12292
  42.7 33.1 %copy-start.6 = (bf16[8,256,256]{2,1,0:T(8,128)(2,1)S(1)}, bf16[8,256,256]{2,1,0:T(8,128)(2,1)}, u32[]{:S(2)}) copy-start(bf16[8,256,256]{2,1,0:T(8,128)(2,1)} %param.5) | copy-start | bytes 3145732
  115.9 297.4 %all-gather.6.cloned.1.call-start = ((), (), s32[]{:S(2)}) async-start(), calls=%async_computation.7 | async-start | bytes 4325376 | tf_op jit(solution)/shard_map/all_gather | solution.py:38
  268.7 429.1 %copy-start.1 = (f32[2,8,16,256]{3,1,2,0:T(8,128)}, f32[2,8,16,256]{3,1,2,0:T(8,128)S(1)}, u32[]{:S(2)}) copy-start(f32[2,8,16,256]{3,1,2,0:T(8,128)S(1)} %get-tuple-element.33) | copy-start | bytes 786436
  350.0 738.5 %copy-start.3 = (f32[2,8,16,256]{3,1,2,0:T(8,128)}, f32[2,8,16,256]{3,1,2,0:T(8,128)S(1)}, u32[]{:S(2)}) copy-start(f32[2,8,16,256]{3,1,2,0:T(8,128)S(1)} %get-tuple-element.31) | copy-start | bytes 786436
  350.8 308.4 %reduce-scatter.9.cloned.1.call-start = ((), (), s32[]{:S(2)}) async-start(), calls=%async_computation.8 | async-start | bytes 8650752 | tf_op jit(solution)/shard_map/reduce_scatter | solution.py:32
  512.3 291.5 %all-gather.8.cloned.1.call-start = ((), (), s32[]{:S(2)}) async-start(), calls=%async_computation.9 | async-start | bytes 4325376 | tf_op jit(solution)/shard_map/all_gather | solution.py:38
  741.4 308.4 %reduce-scatter.11.cloned.1.call-start = ((), (), s32[]{:S(2)}) async-start(), calls=%async_computation.10 | async-start | bytes 8650752 | tf_op jit(solution)/shard_map/reduce_scatter | solution.py:32
  902.9 291.6 %all-gather.10.cloned.1.call-start = ((), (), s32[]{:S(2)}) async-start(), calls=%async_computation.11 | async-start | bytes 4325376 | tf_op jit(solution)/shard_map/all_gather | solution.py:38
  1132.0 308.8 %reduce-scatter.13.cloned.1.call-start = ((), (), s32[]{:S(2)}) async-start(), calls=%async_computation.12 | async-start | bytes 8650752 | tf_op jit(solution)/shard_map/reduce_scatter | solution.py:32
  1293.6 290.9 %all-gather.12.cloned.1.call-start = ((), (), s32[]{:S(2)}) async-start(), calls=%async_computation.13 | async-start | bytes 4325376 | tf_op jit(solution)/shard_map/all_gather | solution.py:38
  1521.9 308.4 %reduce-scatter.15.cloned.1.call-start = ((), (), s32[]{:S(2)}) async-start(), calls=%async_computation.14 | async-start | bytes 8650752 | tf_op jit(solution)/shard_map/reduce_scatter | solution.py:32
  1683.5 290.5 %all-gather.14.cloned.1.call-start = ((), (), s32[]{:S(2)}) async-start(), calls=%async_computation.15 | async-start | bytes 4325376 | tf_op jit(solution)/shard_map/all_gather | solution.py:38
  1911.4 308.3 %reduce-scatter.17.cloned.1.call-start = ((), (), s32[]{:S(2)}) async-start(), calls=%async_computation.16 | async-start | bytes 8650752 | tf_op jit(solution)/shard_map/reduce_scatter | solution.py:32
  2032.8 40.1 %copy-start.7 = (f32[2,1]{0,1:T(1,128)S(1)}, f32[2,1]{0,1:T(1,128)}, u32[]{:S(2)}) copy-start(f32[2,1]{0,1:T(1,128)} %get-tuple-element.56) | copy-start | bytes 28
  2032.8 40.2 %copy-start.8 = (f32[2,1]{0,1:T(1,128)S(1)}, f32[2,1]{0,1:T(1,128)}, u32[]{:S(2)}) copy-start(f32[2,1]{0,1:T(1,128)} %get-tuple-element.44) | copy-start | bytes 28
  2032.8 40.3 %copy-start.2 = (f32[2,8,16,256]{3,1,2,0:T(8,128)S(1)}, f32[2,8,16,256]{3,1,2,0:T(8,128)}, u32[]{:S(2)}) copy-start(f32[2,8,16,256]{3,1,2,0:T(8,128)} %copy-done.1) | copy-start | bytes 786436
  2032.8 41.1 %copy-start.4 = (f32[2,8,16,256]{3,1,2,0:T(8,128)S(1)}, f32[2,8,16,256]{3,1,2,0:T(8,128)}, u32[]{:S(2)}) copy-start(f32[2,8,16,256]{3,1,2,0:T(8,128)} %copy-done.3) | copy-start | bytes 786436
  2032.8 41.8 %copy-start.9 = (f32[2,1]{0,1:T(1,128)S(1)}, f32[2,1]{0,1:T(1,128)}, u32[]{:S(2)}) copy-start(f32[2,1]{0,1:T(1,128)} %get-tuple-element.54) | copy-start | bytes 28
  2032.8 41.9 %copy-start.10 = (f32[2,1]{0,1:T(1,128)S(1)}, f32[2,1]{0,1:T(1,128)}, u32[]{:S(2)}) copy-start(f32[2,1]{0,1:T(1,128)} %get-tuple-element.42) | copy-start | bytes 28
  2032.8 42.7 %copy-start.11 = (f32[2,1]{0,1:T(1,128)S(1)}, f32[2,1]{0,1:T(1,128)}, u32[]{:S(2)}) copy-start(f32[2,1]{0,1:T(1,128)} %get-tuple-element.52) | copy-start | bytes 28
  2032.8 42.8 %copy-start.12 = (f32[2,1]{0,1:T(1,128)S(1)}, f32[2,1]{0,1:T(1,128)}, u32[]{:S(2)}) copy-start(f32[2,1]{0,1:T(1,128)} %get-tuple-element.40) | copy-start | bytes 28
Sparse Core Ops, SparseCore 0:
  116.0 151.3 reduce-scatter.6
  350.9 62.3 all-gather.5
  512.5 146.6 reduce-scatter.8
  741.5 62.3 all-gather.7
  903.1 146.6 reduce-scatter.10
  1132.1 62.3 all-gather.9
  1293.7 147.0 reduce-scatter.12
  1522.0 62.3 all-gather.11
  1683.6 146.6 reduce-scatter.14
  1911.6 62.3 all-gather.13
  2073.0 146.6 reduce-scatter.16
where the time goes:
time: 2320 us; the launch traced here: 2310 us
  waiting for transfers between devices  1190 us (51%)
  matrix products  524 us (23%)
  blocking collectives  467 us (20%)
  local copies, waits for them, and re-layouts  84.7 us (4%)
  other arithmetic  29.3 us (1%)
    reduce_scatter x6, waiting for transfers between devices, device_fn(): lax.psum_scatter(part_sigma, 'terms', scatter_dimension=1, tiled=True)  880 us
    all_gather x5, waiting for transfers between devices, device_fn(): lax.all_gather(v_next.astype(jnp.bfloat16), 'terms', axis=1, tiled=True)  312 us
    psum x6, blocking collectives, device_fn(): lax.psum(jnp.sum(residual * residual, axis=(1, 2, 3)), 'terms') / n_elems  246 us
    psum x6, blocking collectives, device_fn(): alpha = lax.psum(jnp.sum(sigma * v_cur, axis=(1, 2, 3)), 'terms') / n_elems  222 us
    dot_general x6, matrix products, device_fn(): jnp.einsum('kqu,krcub->krcqb', phys_loc, right_part, preferred_element_ty...  198 us
    dot_general x6, matrix products, device_fn(): jnp.einsum('kac,krcqb->raqb', left_loc, mid_part, preferred_element_type=...  179 us
    dot_general x6, matrix products, device_fn(): jnp.einsum('rcup,kbp->krcub', v_in, right_loc, preferred_element_type=jnp...  146 us
    transpose x6, local copies, waits for them, and re-layouts, device_fn(): jnp.einsum('kac,krcqb->raqb', left_loc, mid_part, preferred_element_type=...  61.9 us
  transfers between devices with their start and end apart: 11, of which 11 were waited for; matrix products, arithmetic and copies ran while one was open for 0% of the time, Pallas kernels for 0%

commit v1 on v0

v1 whole, which is shorter than its diff:
```python
import functools

import jax
import jax.numpy as jnp
from jax import lax
from jax.experimental import pallas as pl
from jax.experimental.pallas import tpu as pltpu
from jax.sharding import PartitionSpec as P

STEPS = 6
BF = jnp.bfloat16
F32 = jnp.float32
MESH = pl.DeviceIdType.MESH
VM = pltpu.VMEM
N_ELEMS = 256 * 16 * 256


def rcopy(src, dst, ss, rs, dev):
    return pltpu.make_async_remote_copy(src_ref=src, dst_ref=dst, send_sem=ss, recv_sem=rs, device_id=(dev,), device_id_type=MESH)


def greet(devs):
    bar = pltpu.get_barrier_semaphore()
    for d in devs:
        pl.semaphore_signal(bar, inc=1, device_id=(d,), device_id_type=MESH)
    pl.semaphore_wait(bar, len(devs))


def setup_kernel(l_ref, r_ref, w_ref, la, ra, wa, ls, zs, xs, ys, rsl, rss, rrs, wss, wrs):
    me = lax.axis_index("terms")
    c = lax.rem(me, 2)
    s = me // 2
    z = me // 8
    xn, yn = me ^ 2, me ^ 4
    sx, sy = s ^ 1, s ^ 2
    peers = [lax.rem(me + 2 * d, 32) for d in range(1, 16)]
    greet(peers)

    def half(ref, src, h):
        return ref.at[src, pl.ds(4 * h, 4)]

    own = [pltpu.make_async_copy(l_ref, la.at[s], ls.at[0]),
           pltpu.make_async_copy(r_ref.at[:, pl.ds(32 * lax.rem(s, 8), 32)], ra.at[s], ls.at[1]),
           pltpu.make_async_copy(w_ref, wa.at[s], ls.at[2])]
    for o in own:
        o.start()
    sends = []

    def send_z(src, k, mine, up):
        cond = (z < 3) if up else (z > 0)
        dev = me + 8 if up else me - 8
        for h in range(2):
            ref = l_ref.at[pl.ds(4 * h, 4)] if mine else half(la, src, h)
            cp = rcopy(ref, half(la, src, h), zs.at[0 if up else 1, k, h], rsl.at[src, h], dev)
            yield cp, cond

    def run_z(src, k, mine, up, guard):
        for cp, cond in send_z(src, k, mine, up):
            cc = cond if guard is None else jnp.logical_and(cond, guard)
            pl.when(cc)(cp.start)
            sends.append((cp, cc))

    def run_xy(src, k, mine, guard):
        for h, dev, sem in ((0, xn, xs.at[k]), (1, yn, ys.at[k]), (0, yn, ys.at[4 + k]), (1, xn, xs.at[4 + k])):
            ref = l_ref.at[pl.ds(4 * h, 4)] if mine else half(la, src, h)
            cp = rcopy(ref, half(la, src, h), sem, rsl.at[src, h], dev)
            if guard is None:
                cp.start()
            else:
                pl.when(guard)(cp.start)
            sends.append((cp, guard))

    def wait_in(src, h, guard):
        cp = rcopy(half(la, src, h), half(la, src, h), xs.at[0], rsl.at[src, h], xn)
        if guard is None:
            cp.wait_recv()
        else:
            pl.when(guard)(cp.wait_recv)

    def forward(srcx, srcy, k, guard):
        for src, h, dev, sem in ((srcx, 0, yn, ys.at[8 + k]), (srcy, 1, xn, xs.at[8 + k])):
            wait_in(src, h, guard)
            cp = rcopy(half(la, src, h), half(la, src, h), sem, rsl.at[src, h], dev)
            if guard is None:
                cp.start()
            else:
                pl.when(guard)(cp.start)
            sends.append((cp, guard))

    run_z(s, 0, True, True, None)
    run_z(s, 0, True, False, None)
    run_xy(s, 0, True, None)
    for d in range(1, 16):
        dst = lax.rem(s + d, 16)
        rsem = lax.rem(16 - d, 16)
        dev = 2 * dst + c
        cp = rcopy(r_ref.at[:, pl.ds(32 * lax.rem(dst, 8), 32)], ra.at[s], rss.at[d], rrs.at[rsem], dev)
        cp.start()
        sends.append((cp, "r"))
        cp = rcopy(w_ref, wa.at[s], wss.at[d], wrs.at[rsem], dev)
        cp.start()
        sends.append((cp, "r"))
    forward(sx, sy, 0, None)
    slot = [(1, -1), (1, 1), (2, -1), (2, 1), (3, -1), (3, 1)]
    pend = []
    for n, (e, sign) in enumerate(slot):
        guard = (z >= e) if sign < 0 else (z <= 3 - e)
        src = jnp.clip(s + 4 * e * sign, 0, 15)
        for h in range(2):
            wait_in(src, h, guard)
        if e < 3:
            run_z(src, e, False, sign < 0, guard)
        pend.append((src, sign, e, guard))
        k = jnp.where(sign < 0, z - e, z + e - 1)
        k = 1 + jnp.clip(k, 0, 2)
        run_xy(src, k, False, guard)
        forward(src ^ 1, src ^ 2, k, guard)
    for n in range(4):
        base = lax.rem(s, 4) + 4 * n
        wait_in(base ^ 1, 1, None)
        wait_in(base ^ 2, 0, None)
        wait_in(base ^ 3, 0, None)
        wait_in(base ^ 3, 1, None)
    for cp, guard in sends:
        if guard is None:
            cp.wait_send()
        elif isinstance(guard, str):
            cp.wait_send()
            cp.wait_recv()
        else:
            pl.when(guard)(cp.wait_send)
    for o in own:
        o.wait()


def setup(l_loc, r_loc, w_loc):
    any_ = pl.BlockSpec(memory_space=pl.ANY)
    vm = pl.BlockSpec(memory_space=VM)
    dma = pltpu.SemaphoreType.DMA
    return pl.pallas_call(
        setup_kernel,
        out_shape=(jax.ShapeDtypeStruct((16, 8, 256, 256), BF), jax.ShapeDtypeStruct((16, 8, 32, 256), BF), jax.ShapeDtypeStruct((16, 16, 128), BF)),
        in_specs=[vm, vm, vm],
        out_specs=(any_, any_, any_),
        scratch_shapes=[dma((3,)), dma((2, 3, 2)), dma((12,)), dma((12,)), dma((16, 2)), dma((16,)), dma((16,)), dma((16,)), dma((16,))],
        compiler_params=pltpu.CompilerParams(collective_id=0, has_side_effects=True, vmem_limit_bytes=24 * 2**20),
    )(l_loc, r_loc, w_loc)


def kron_kernel(w_ref, o_ref):
    row = lax.broadcasted_iota(jnp.int32, (16, 256), 0)
    lane = lax.broadcasted_iota(jnp.int32, (16, 256), 1)
    mask = (lane & 15) == row
    for k in range(8):
        for q in range(16):
            v = jnp.broadcast_to(w_ref[k, q:q + 1, :], (16, 256))
            o_ref[k, q * 16:(q + 1) * 16, :] = jnp.where(mask, v, 0.0).astype(BF)


def kron(wexp):
    terms = wexp.shape[0]
    return pl.pallas_call(
        kron_kernel, grid=(terms // 8,),
        in_specs=[pl.BlockSpec((8, 16, 256), lambda i: (i, 0, 0))],
        out_specs=pl.BlockSpec((8, 256, 256), lambda i: (i, 0, 0)),
        out_shape=jax.ShapeDtypeStruct((terms, 256, 256), BF),
    )(wexp)


KC = 8


def matvec_kernel(u_ref, r_ref, w_ref, l_ref, o_ref, y, zz):
    @pl.when(pl.program_id(0) == 0)
    def _():
        o_ref[...] = jnp.zeros_like(o_ref)

    rb = r_ref[...].reshape(KC * 32, 256)
    for u in range(16):
        yu = jnp.dot(rb, u_ref[u], preferred_element_type=F32).astype(BF).reshape(KC, 2, 16, 256)
        for t in range(2):
            y[:, u * 16:(u + 1) * 16, t * 256:(t + 1) * 256] = yu[:, t]
    for k in range(KC):
        zk = jnp.dot(w_ref[k], y[k], preferred_element_type=F32).astype(BF)
        for t in range(2):
            zz[t * 256:(t + 1) * 256, k * 256:(k + 1) * 256] = zk[:, t * 256:(t + 1) * 256]
    o_ref[...] += jnp.dot(zz[...], l_ref[...].reshape(KC * 256, 256), preferred_element_type=F32)


def matvec(u, r, w, l):
    terms = l.shape[0]
    return pl.pallas_call(
        matvec_kernel, grid=(terms // KC,),
        in_specs=[pl.BlockSpec((16, 256, 256), lambda i: (0, 0, 0)), pl.BlockSpec((KC, 32, 256), lambda i: (i, 0, 0)),
                  pl.BlockSpec((KC, 256, 256), lambda i: (i, 0, 0)), pl.BlockSpec((KC, 256, 256), lambda i: (i, 0, 0))],
        out_specs=pl.BlockSpec((512, 256), lambda i: (0, 0)),
        out_shape=jax.ShapeDtypeStruct((512, 256), F32),
        scratch_shapes=[VM((KC, 256, 512), BF), VM((512, KC * 256), BF)],
        compiler_params=pltpu.CompilerParams(vmem_limit_bytes=40 * 2**20),
    )(u, r, w, l)


def update_kernel(last, part, v_ref, vp_ref, bp_ref, vn_ref, u_ref, ab_ref, got, sc_out, sc_in, ps, sss, srs, uss, urs, fss):
    me = lax.axis_index("terms")
    c = lax.rem(me, 2)
    half = me // 16
    m = lax.rem(me, 16)
    sib = me ^ 1
    others = [16 * half + (m ^ d) for d in range(1, 16)]
    greet(others)
    swap = rcopy(part.at[1 - c], got, ps.at[0], ps.at[1], sib)
    swap.start()
    swap.wait()
    v = v_ref[...]
    w = part[c] + got[...]
    w2 = w - bp_ref[1:2, 0:1] * vp_ref[...]
    s1 = jnp.sum(w * v)
    s4 = jnp.sum(v * v)
    sh = jnp.sum(w2 * v) / jnp.where(s4 > 0, s4, 1.0)
    w3 = w2 - sh * v
    s2 = jnp.sum(w3 * w3)
    s3 = jnp.sum(w3 * v)
    row = lax.broadcasted_iota(jnp.int32, (8, 128), 0)
    tile = jnp.zeros((8, 128), F32)
    for n, val in enumerate((s1, s2, s3, s4, sh)):
        tile = jnp.where(row == n, val, tile)
    sc_out[...] = tile
    sc_in[m] = tile
    sends = []
    for d in range(1, 16):
        cp = rcopy(sc_out, sc_in.at[m], sss.at[d], srs.at[d], others[d - 1])
        cp.start()
        sends.append(cp)
    for cp in sends:
        cp.wait()
    alpha = jnp.zeros((1, 1), F32)
    for d in range(16):
        alpha = alpha + sc_in[d, 0:1, 0:1]
    alpha = alpha / N_ELEMS
    beta2 = jnp.zeros((1, 1), F32)
    for d in range(16):
        dl = alpha - sc_in[d, 4:5, 0:1]
        beta2 = beta2 + (sc_in[d, 1:2, 0:1] - 2.0 * dl * sc_in[d, 2:3, 0:1] + dl * dl * sc_in[d, 3:4, 0:1])
    beta = jnp.sqrt(jnp.maximum(beta2, 0.0) / N_ELEMS)
    ab_ref[...] = jnp.where(row == 0, jnp.broadcast_to(alpha, (8, 128)), jnp.broadcast_to(beta, (8, 128)))
    vn = (w2 - alpha * v) / beta
    b0 = 16 * m

    def mine(src):
        return u_ref.at[:, pl.ds(16 * src, 16), :]

    if not last:
        u_ref[:, pl.ds(b0, 16), :] = vn.astype(BF).reshape(16, 16, 256)
    vn_ref[...] = vn
    if not last:
        sends = []
        for d in range(1, 16):
            if d == 1 or d % 2 == 0:
                cp = rcopy(mine(m), mine(m), uss.at[d], urs.at[d], others[d - 1])
                cp.start()
                sends.append((d, cp))
        for d, cp in sends[1:]:
            cp.wait_recv()
            fw = rcopy(mine(m ^ d), mine(m ^ d), fss.at[d], urs.at[d + 1], sib)
            fw.start()
            sends.append((d + 1, fw))
        sends[0][1].wait_recv()
        for d, cp in sends[8:]:
            cp.wait_recv()
        for d, cp in sends:
            cp.wait_send()


def update(part, v, vp, bp, last):
    vm = pl.BlockSpec(memory_space=VM)
    dma = pltpu.SemaphoreType.DMA
    return pl.pallas_call(
        functools.partial(update_kernel, last),
        out_shape=(jax.ShapeDtypeStruct((256, 256), F32), jax.ShapeDtypeStruct((16, 256, 256), BF), jax.ShapeDtypeStruct((8, 128), F32)),
        in_specs=[vm] * 4,
        out_specs=(vm, vm, vm),
        scratch_shapes=[VM((256, 256), F32), VM((8, 128), F32), VM((16, 8, 128), F32), dma((2,)), dma((16,)), dma((16,)), dma((16,)), dma((16,)), dma((16,))],
        compiler_params=pltpu.CompilerParams(collective_id=2 if last else 1, has_side_effects=True, vmem_limit_bytes=24 * 2**20),
    )(part.reshape(2, 256, 256), v, vp, bp)


def finish_kernel(v0_ref, *refs):
    vs = refs[:STEPS]
    abs_ = refs[STEPS:2 * STEPS]
    o_ref, ab_ref, tb, rx, ss, rs, xs = refs[2 * STEPS:]
    me = lax.axis_index("terms")
    half = me // 16
    row = lax.broadcasted_iota(jnp.int32, (8, 128), 0)
    lane = lax.broadcasted_iota(jnp.int32, (8, 128), 1)
    tile = jnp.zeros((8, 128), F32)
    for j in range(STEPS):
        tb[j] = vs[j][...].T
        tile = jnp.where(lane == j, abs_[j][...], tile)
    ab_ref[half] = tile
    greet([me ^ d for d in range(1, 32)])
    sends = []
    cross = rcopy(ab_ref.at[half], ab_ref.at[half], xs.at[0], xs.at[1], me ^ 16)
    cross.start()
    for d in range(31, 0, -1):
        p = me ^ d
        cp = rcopy(tb.at[:, pl.ds(pl.multiple_of(8 * p, 8), 8), :], rx.at[me], ss.at[d], rs.at[d], p)
        cp.start()
        sends.append(cp)
    for r in range(2):
        o_ref[r, 0] = v0_ref[r]
    rx[me] = tb[:, pl.ds(pl.multiple_of(8 * me, 8), 8), :]
    for cp in sends:
        cp.wait()
    cross.wait()
    grp = lax.broadcasted_iota(jnp.int32, (8, 128), 1) // 16

    def body(n, carry):
        r = n // STEPS
        j = lax.rem(n, STEPS)
        for h in range(2):
            for hb in range(2):
                xv = [rx[16 * r + 8 * hb + q, j, :, h * 128:(h + 1) * 128] for q in range(8)]
                for d in (1, 2, 4):
                    low = (grp & d) == 0
                    for a in range(8):
                        if a & d == 0:
                            p, q = xv[a], xv[a + d]
                            xv[a] = jnp.where(low, p, pltpu.roll(q, 16 * d, 1))
                            xv[a + d] = jnp.where(low, pltpu.roll(p, 128 - 16 * d, 1), q)
                for q in range(8):
                    o_ref[r, j + 1, :, h * 8 + q, hb * 128:(hb + 1) * 128] = xv[q]
        return carry

    lax.fori_loop(0, 2 * STEPS, body, 0)


def finish(v0rows, vs, abs_):
    vm = pl.BlockSpec(memory_space=VM)
    dma = pltpu.SemaphoreType.DMA
    return pl.pallas_call(
        finish_kernel,
        out_shape=(jax.ShapeDtypeStruct((2, STEPS + 1, 8, 16, 256), F32), jax.ShapeDtypeStruct((2, 8, 128), F32)),
        in_specs=[vm] * (1 + 2 * STEPS),
        out_specs=(vm, vm),
        scratch_shapes=[VM((STEPS, 256, 256), F32), VM((32, STEPS, 8, 256), F32), dma((32,)), dma((32,)), dma((2,))],
        compiler_params=pltpu.CompilerParams(collective_id=3, has_side_effects=True, vmem_limit_bytes=40 * 2**20),
    )(v0rows, *vs, *abs_)


def solution(mesh):
    def device_fn(psi, l_loc, w_loc, r_loc):
        me = lax.axis_index("terms")
        half = me // 16
        m = lax.rem(me, 16)
        la, ra, wa = setup(l_loc, r_loc, w_loc.reshape(16, 128))
        la = la.reshape(128, 256, 256)
        ra = ra.reshape(128, 32, 256)
        wk = kron(jnp.repeat(wa.reshape(128, 16, 16).astype(F32), 16, axis=-1))
        psi = psi.reshape(2, 256, 16, 256)
        norms = jnp.sqrt(jnp.sum(psi * psi, axis=(1, 2, 3)) / N_ELEMS)
        v0rows = lax.dynamic_slice_in_dim(psi, 8 * me, 8, axis=1) / norms[:, None, None, None]
        mine = lax.dynamic_index_in_dim(psi, half, 0, keepdims=False)
        norm = lax.dynamic_index_in_dim(norms, half, 0, keepdims=False)
        u = (mine / norm).astype(BF).transpose(1, 2, 0)
        v = (lax.dynamic_slice_in_dim(mine, 16 * m, 16, axis=2) / norm).transpose(1, 2, 0).reshape(256, 256)
        vp = jnp.zeros_like(v)
        ab = jnp.zeros((8, 128), F32)
        vs, abs_ = [], []
        for j in range(STEPS):
            part = matvec(u, ra, wk, la)
            vn, u, ab = update(part, v, vp, ab, j == STEPS - 1)
            vs.append(vn)
            abs_.append(ab)
            vp, v = v, vn
        vecs, abo = finish(v0rows, vs, abs_)
        return vecs.reshape(2, STEPS + 1, 8, 4, 4, 256), abo[:, 0, :STEPS], abo[:, 1, :STEPS]

    return jax.shard_map(device_fn, mesh=mesh, in_specs=(P(), P("terms"), P("terms"), P("terms")),
                         out_specs=(P(None, None, "terms"), P(), P()), check_vma=False)
```

time: 2320 us -> 604 us (0.26)
  waiting for transfers between devices: 1190 us -> 0 us
  Pallas kernels: 0 us -> 552 us
  matrix products: 524 us -> 0 us
  blocking collectives: 467 us -> 0 us
  local copies, waits for them, and re-layouts: 84.7 us -> 35.8 us
    reduce_scatter x6 -> x0, waiting for transfers between devices: 880 us -> none  [device_fn(): lax.psum_scatter(part_sigma, 'terms', scatter_dimension=1, tiled=True)]
    pallas_call x0 -> x15, Pallas kernels: none -> 552 us  [the longest x6 194 us: matvec(): pl.pallas_call(matvec_kernel, grid=(terms // KC,), in_specs=[pl.BlockSpec...]
    dot_general x18 -> x0, matrix products: 524 us -> none  [the longest x6 198 us: device_fn(): jnp.einsum('kqu,krcub->krcqb', phys_loc, right_part, preferred_element_ty...]
    psum x12 -> x0, blocking collectives: 467 us -> none  [the longest x6 246 us: device_fn(): lax.psum(jnp.sum(residual * residual, axis=(1, 2, 3)), 'terms') / n_elems]
    all_gather x5 -> x0, waiting for transfers between devices: 312 us -> none  [device_fn(): lax.all_gather(v_next.astype(jnp.bfloat16), 'terms', axis=1, tiled=True)]
    transpose x6 -> x2, local copies, waits for them, and re-layouts: 61.9 us -> 5.3 us  [the longest x1 4.3 us: device_fn(): u = (mine / norm).astype(BF).transpose(1, 2, 0)]
  transfers between devices with their start and end apart: 11 -> 0, of which waited for: 11 -> 0; matrix products, arithmetic and copies ran while one was open for 0% -> 0% of each run, Pallas kernels for 0% -> 0%
where the time goes in v1:
time: 604 us; the launch traced here: 603 us
  Pallas kernels  552 us (91%)
  local copies, waits for them, and re-layouts  35.8 us (6%)
  other arithmetic  14.9 us (2%)
    pallas_call x6, Pallas kernels, matvec(): pl.pallas_call(matvec_kernel, grid=(terms // KC,), in_specs=[pl.BlockSpec...  194 us
    pallas_call x1, Pallas kernels, setup(): pl.pallas_call(setup_kernel, out_shape=(jax.ShapeDtypeStruct((16, 8, 256,...  167 us
    pallas_call x6, Pallas kernels, update(): pl.pallas_call(functools.partial(update_kernel, last), out_shape=(jax.Sha...  135 us
    pallas_call x1, Pallas kernels, finish(): pl.pallas_call(finish_kernel, out_shape=(jax.ShapeDtypeStruct((2, STEPS +...  44 us
    pallas_call x1, Pallas kernels, kron(): pl.pallas_call(kron_kernel, grid=(terms // 8,), in_specs=[pl.BlockSpec((8...  12.3 us

profile of v1, /device:TPU:0, one launch (start us, length us, event | category | flops | bytes accessed | tf_op | source)
XLA Modules:
  0.0 603.5 jit_solution(12429909212386355427)
XLA Ops:
  0.7 5.7 multiply_reduce_fusion
  6.3 0.6 dynamic_slice.16
  7.0 10.2 %reshape.58 = f32[2,256,16,256]{3,2,1,0:T(8,128)} reshape(f32[2,256,4,4,256]{4,3,2,1,0:T(4,128)} %param.4) | data formatting | bytes 16777216 | tf_op jit(solution)/shard_map/reshape | solution.py:359
  17.2 1.0 dynamic-slice_divide_fusion.v0_ref
  18.3 3.4 divide_bitcast_fusion
  21.7 4.8 fusion
  26.5 1.0 copy.13
  27.5 4.3 copy.12.u_ref
  31.8 1.2 copy-done.2
  33.0 1.2 copy-done.3
  34.2 166.5 %shard_map.67 = (bf16[16,8,256,256]{3,2,1,0:T(8,128)(2,1)S(1)}, bf16[16,8,32,256]{3,2,1,0:T(8,128)(2,1)S(1)}, bf16[16,16,128]{2,1,0:T(8,128)(2,1)S(1)}) custom-call(bf16[8,256,256]{2,1,0:T(8,128)(2,1)S(1)} %copy-done.2, bf16[8,256,256]{2,1,0:T(8,128)(2,1)S(1)} %copy-done.3, bf16[16,128]{1,0:T(8,128)(2,1)S(1)} %reshape.59.w_ref), custom_call_target="tpu_custom_call" | custom-call | tf_op jit(solution)/shard_map/pallas_call | solution.py:140
  200.8 5.7 copy-done
  206.5 1.3 reshape.71
  207.8 1.6 copy.10
  209.4 1.5 broadcast_in_dim.10
  210.9 3.2 copy.11.w_ref
  214.1 12.3 %shard_map.68.w_ref = bf16[128,256,256]{2,1,0:T(8,128)(2,1)} custom-call(f32[128,16,256]{2,1,0:T(8,128)} %copy.11.w_ref), custom_call_target="tpu_custom_call" | custom-call | tf_op jit(solution)/shard_map/pallas_call | solution.py:162
  226.4 1.6 copy-done.1
  228.0 32.3 %shard_map.69 = f32[512,256]{1,0:T(8,128)S(1)} custom-call(bf16[16,256,256]{2,1,0:T(8,128)(2,1)S(1)} %copy-done.1, bf16[128,32,256]{2,1,0:T(8,128)(2,1)S(1)} %bitcast.29, bf16[128,256,256]{2,1,0:T(8,128)(2,1)} %shard_map.68.w_ref, bf16[128,256,256]{2,1,0:T(8,128)(2,1)} %bitcast.23), custom_call_target="tpu_custom_call" | custom-call | tf_op jit(solution)/shard_map/pallas_call | solution.py:192
  260.3 24.7 %shard_map.70 = (f32[256,256]{1,0:T(8,128)S(1)}, bf16[16,256,256]{2,1,0:T(8,128)(2,1)S(1)}, f32[8,128]{1,0:T(8,128)S(1)}) custom-call(f32[2,256,256]{2,1,0:T(8,128)S(1)} %bitcast.37, f32[256,256]{1,0:T(8,128)S(1)} %bitcast.35, f32[256,256]{1,0:T(8,128)S(1)} %broadcast_in_dim.11.vp_ref, f32[8,128]{1,0:T(8,128)S(1)} %broadcast_in_dim.12.bp_ref), custom_call_target="tpu_custom_call" | custom-call | tf_op jit(solution)/shard_map/pallas_call | solution.py:277
  285.0 32.3 %shard_map.71 = f32[512,256]{1,0:T(8,128)S(1)} custom-call(bf16[16,256,256]{2,1,0:T(8,128)(2,1)S(1)} %get-tuple-element.29.u_ref, bf16[128,32,256]{2,1,0:T(8,128)(2,1)S(1)} %bitcast.30, bf16[128,256,256]{2,1,0:T(8,128)(2,1)} %shard_map.68.w_ref, bf16[128,256,256]{2,1,0:T(8,128)(2,1)} %bitcast.24), custom_call_target="tpu_custom_call" | custom-call | tf_op jit(solution)/shard_map/pallas_call | solution.py:192
  317.4 25.5 %shard_map.72 = (f32[256,256]{1,0:T(8,128)S(1)}, bf16[16,256,256]{2,1,0:T(8,128)(2,1)S(1)}, f32[8,128]{1,0:T(8,128)S(1)}) custom-call(f32[2,256,256]{2,1,0:T(8,128)S(1)} %bitcast.39, f32[256,256]{1,0:T(8,128)S(1)} %get-tuple-element.28.v_ref.vp_ref.refs_0_, f32[256,256]{1,0:T(8,128)S(1)} %bitcast.36, f32[8,128]{1,0:T(8,128)S(1)} %get-tuple-element.30.bp_ref.refs_6_), custom_call_target="tpu_custom_call" | custom-call | tf_op jit(solution)/shard_map/pallas_call | solution.py:277
  342.9 32.5 %shard_map.73 = f32[512,256]{1,0:T(8,128)S(1)} custom-call(bf16[16,256,256]{2,1,0:T(8,128)(2,1)S(1)} %get-tuple-element.32.u_ref, bf16[128,32,256]{2,1,0:T(8,128)(2,1)S(1)} %bitcast.31, bf16[128,256,256]{2,1,0:T(8,128)(2,1)} %shard_map.68.w_ref, bf16[128,256,256]{2,1,0:T(8,128)(2,1)} %bitcast.25), custom_call_target="tpu_custom_call" | custom-call | tf_op jit(solution)/shard_map/pallas_call | solution.py:192
  375.4 24.9 %shard_map.74 = (f32[256,256]{1,0:T(8,128)S(1)}, bf16[16,256,256]{2,1,0:T(8,128)(2,1)S(1)}, f32[8,128]{1,0:T(8,128)S(1)}) custom-call(f32[2,256,256]{2,1,0:T(8,128)S(1)} %bitcast.40, f32[256,256]{1,0:T(8,128)S(1)} %get-tuple-element.31.v_ref.vp_ref.refs_1_, f32[256,256]{1,0:T(8,128)S(1)} %get-tuple-element.28.v_ref.vp_ref.refs_0_, ...), custom_call_target="tpu_custom_call" | custom-call | tf_op jit(solution)/shard_map/pallas_call | solution.py:277
  400.3 32.2 %shard_map.75 = f32[512,256]{1,0:T(8,128)S(1)} custom-call(bf16[16,256,256]{2,1,0:T(8,128)(2,1)S(1)} %get-tuple-element.35.u_ref, bf16[128,32,256]{2,1,0:T(8,128)(2,1)S(1)} %bitcast.32, bf16[128,256,256]{2,1,0:T(8,128)(2,1)} %shard_map.68.w_ref, bf16[128,256,256]{2,1,0:T(8,128)(2,1)} %bitcast.26), custom_call_target="tpu_custom_call" | custom-call | tf_op jit(solution)/shard_map/pallas_call | solution.py:192
  432.5 25.7 %shard_map.76 = (f32[256,256]{1,0:T(8,128)S(1)}, bf16[16,256,256]{2,1,0:T(8,128)(2,1)S(1)}, f32[8,128]{1,0:T(8,128)S(1)}) custom-call(f32[2,256,256]{2,1,0:T(8,128)S(1)} %bitcast.41, f32[256,256]{1,0:T(8,128)S(1)} %get-tuple-element.34.v_ref.vp_ref.refs_2_, f32[256,256]{1,0:T(8,128)S(1)} %get-tuple-element.31.v_ref.vp_ref.refs_1_, ...), custom_call_target="tpu_custom_call" | custom-call | tf_op jit(solution)/shard_map/pallas_call | solution.py:277
  458.2 32.2 %shard_map.77 = f32[512,256]{1,0:T(8,128)S(1)} custom-call(bf16[16,256,256]{2,1,0:T(8,128)(2,1)S(1)} %get-tuple-element.38.u_ref, bf16[128,32,256]{2,1,0:T(8,128)(2,1)S(1)} %bitcast.33, bf16[128,256,256]{2,1,0:T(8,128)(2,1)} %shard_map.68.w_ref, bf16[128,256,256]{2,1,0:T(8,128)(2,1)} %bitcast.27), custom_call_target="tpu_custom_call" | custom-call | tf_op jit(solution)/shard_map/pallas_call | solution.py:192
  490.4 25.0 %shard_map.78 = (f32[256,256]{1,0:T(8,128)S(1)}, bf16[16,256,256]{2,1,0:T(8,128)(2,1)S(1)}, f32[8,128]{1,0:T(8,128)S(1)}) custom-call(f32[2,256,256]{2,1,0:T(8,128)S(1)} %bitcast.42, f32[256,256]{1,0:T(8,128)S(1)} %get-tuple-element.37.v_ref.vp_ref.refs_3_, f32[256,256]{1,0:T(8,128)S(1)} %get-tuple-element.34.v_ref.vp_ref.refs_2_, ...), custom_call_target="tpu_custom_call" | custom-call | tf_op jit(solution)/shard_map/pallas_call | solution.py:277
  515.4 32.2 %shard_map.79 = f32[512,256]{1,0:T(8,128)S(1)} custom-call(bf16[16,256,256]{2,1,0:T(8,128)(2,1)S(1)} %get-tuple-element.41.u_ref, bf16[128,32,256]{2,1,0:T(8,128)(2,1)S(1)} %bitcast.34, bf16[128,256,256]{2,1,0:T(8,128)(2,1)} %shard_map.68.w_ref, bf16[128,256,256]{2,1,0:T(8,128)(2,1)} %bitcast.28), custom_call_target="tpu_custom_call" | custom-call | tf_op jit(solution)/shard_map/pallas_call | solution.py:192
  547.6 9.5 %shard_map.80 = (f32[256,256]{1,0:T(8,128)S(1)}, bf16[16,256,256]{2,1,0:T(8,128)(2,1)}, f32[8,128]{1,0:T(8,128)S(1)}) custom-call(f32[2,256,256]{2,1,0:T(8,128)S(1)} %bitcast.38, f32[256,256]{1,0:T(8,128)S(1)} %get-tuple-element.40.v_ref.refs_4_, f32[256,256]{1,0:T(8,128)S(1)} %get-tuple-element.37.v_ref.vp_ref.refs_3_, ...), custom_call_target="tpu_custom_call" | custom-call | tf_op jit(solution)/shard_map/pallas_call | solution.py:277
  557.1 44.0 %shard_map.81 = (f32[2,7,8,16,256]{4,3,2,1,0:T(8,128)S(1)}, f32[2,8,128]{2,1,0:T(8,128)S(1)}) custom-call(f32[2,8,16,256]{3,2,1,0:T(8,128)S(1)} %dynamic-slice_divide_fusion.v0_ref, f32[256,256]{1,0:T(8,128)S(1)} %get-tuple-element.28.v_ref.vp_ref.refs_0_, f32[256,256]{1,0:T(8,128)S(1)} %get-tuple-element.31.v_ref.vp_ref.refs_1_, ...), custom_call_target="tpu_custom_call" | custom-call | tf_op jit(solution)/shard_map/pallas_call | solution.py:340
  601.1 1.8 reshape.70
  (11 shorter events, 0.7 us)
Async XLA Ops:
  0.7 6.3 %copy-start.4 = (bf16[8,16,16]{2,1,0:T(8,128)(2,1)S(1)}, bf16[8,16,16]{2,1,0:T(8,128)(2,1)}, u32[]{:S(2)}) copy-start(bf16[8,16,16]{2,1,0:T(8,128)(2,1)} %param.6) | copy-start | bytes 12292
  31.8 1.2 copy-start.2
  33.0 1.2 copy-start.3
  200.8 5.7 copy-start
  226.4 1.6 copy-start.1

commit v2 on v0

v2 whole, which is shorter than its diff:
```python
import functools

import jax
import jax.numpy as jnp
from jax import lax
from jax.experimental import pallas as pl
from jax.experimental.pallas import tpu as pltpu
from jax.sharding import PartitionSpec as P

STEPS = 6
KC = 8
BF = jnp.bfloat16
F32 = jnp.float32
MESH = pl.DeviceIdType.MESH
VM = pltpu.VMEM
D, H = 256, 128
N_ELEMS = D * 16 * D
TILE = (8, H)
NEAR = (2, 4, 8, 6, 10, 12, 14)


def rcopy(src, dst, ss, rs, dev):
    return pltpu.make_async_remote_copy(src_ref=src, dst_ref=dst, send_sem=ss, recv_sem=rs, device_id=(dev,), device_id_type=MESH)


def when(cond, fn):
    pl.when(cond)(fn)


def lanczos_kernel(psi, l_ref, w_ref, r_ref, o_ref, ab_ref,
                   lb, kr, rb, wb, ub, y, zz, acc, got, vb, ps, v0b, fk, tb, rx, ost, sc_out, sc_in, nt_out, nt_in, bp,
                   loc, osem, psem, zs, xys, fws, rsl, rss, rsr, wss, wsr, ns, sw, sss, ssr, uss, usr, ufs, oss, osr, cs):
    me = lax.axis_index("terms")
    c = lax.rem(me, 2)
    s = me // 2
    z = me // 8
    half = me // 16
    m = lax.rem(me, 16)
    b0 = pl.multiple_of(16 * m, 16)
    sib = me ^ 1
    xn, yn = me ^ 2, me ^ 4

    own = [pltpu.make_async_copy(l_ref, lb.at[s, :, pl.ds(0, 384)], loc.at[0]),
           pltpu.make_async_copy(r_ref.at[:, pl.ds(pl.multiple_of(32 * lax.rem(s, 8), 32), 32)], rb.at[s], loc.at[1]),
           pltpu.make_async_copy(w_ref, wb.at[s], loc.at[2]),
           pltpu.make_async_copy(psi.at[:, pl.ds(8 * me, 8)], v0b, loc.at[3])]
    for o in own:
        o.start()

    def p_copy(q):
        return pltpu.make_async_copy(psi.at[half, :, q // 4, lax.rem(q, 4), :], ps.at[lax.rem(q, 4)], psem.at[lax.rem(q, 4)])

    for q in range(4):
        p_copy(q).start()

    bar = pltpu.get_barrier_semaphore()
    for d in range(1, 32):
        pl.semaphore_signal(bar, inc=1, device_id=(me ^ d,), device_id_type=MESH)
    pl.semaphore_wait(bar, 31)

    def lh(src, h):
        return lb.at[src, pl.ds(4 * h, 4), pl.ds(0, 384)]

    def w_copy(d):
        return rcopy(w_ref, wb.at[s], wss.at[d], wsr.at[s], me ^ (2 * d))

    def r_copy(d):
        dst = s ^ d
        return rcopy(r_ref.at[:, pl.ds(pl.multiple_of(32 * lax.rem(dst, 8), 32), 32)], rb.at[s], rss.at[d], rsr.at[s], me ^ (2 * d))

    def z_copy(src, g, h, dev, mine=False):
        return rcopy(l_ref.at[pl.ds(4 * h, 4)] if mine else lh(src, h), lh(src, h), zs.at[g, h], rsl.at[src, h], dev)

    def xy_copies(src, g, mine=False):
        out = []
        for n, (h, dev) in enumerate(((0, xn), (1, yn), (0, yn), (1, xn))):
            out.append(rcopy(l_ref.at[pl.ds(4 * h, 4)] if mine else lh(src, h), lh(src, h), xys.at[g, n], rsl.at[src, h], dev))
        return out

    def f_copy(src, g, h):
        return rcopy(lh(src, h), lh(src, h), fws.at[g, h], rsl.at[src, h], yn if h == 0 else xn)

    def wait_l(src, h):
        rcopy(lh(src, h), lh(src, h), zs.at[0, 0], rsl.at[src, h], xn).wait_recv()

    for d in range(1, 16):
        w_copy(d).start()
    for h in range(2):
        when(z < 3, z_copy(s, 0, h, me + 8, True).start)
        when(z > 0, z_copy(s, 4, h, me - 8, True).start)
    for d in range(1, 8):
        r_copy(d).start()
    for cp in xy_copies(s, 0, True):
        cp.start()

    def square(q, t):
        p_copy(q).wait()
        t = lax.fori_loop(0, 32, lambda n, t: t + ps[lax.rem(q, 4), pl.ds(8 * n, 8), :] * ps[lax.rem(q, 4), pl.ds(8 * n, 8), :], t)
        p_copy(lax.rem(q + 4, 16)).start()
        return t

    total = lax.fori_loop(0, 16, square, jnp.zeros((8, D), F32))
    norm = jnp.sqrt(jnp.sum(total) / N_ELEMS)
    nt_out[...] = jnp.full(TILE, norm, F32)
    ncp = rcopy(nt_out, nt_in, ns.at[0], ns.at[1], me ^ 16)
    ncp.start()

    def first(q, carry):
        p_copy(q).wait()
        t = ps[lax.rem(q, 4)].T / norm
        when(q < 12, lambda: p_copy(q + 4).start())
        acc[0] = t
        ub[q] = t.astype(BF)
        vb[0, pl.ds(pl.multiple_of(16 * q, 16), 16), :] = acc[0, pl.ds(b0, 16), :]
        return carry

    lax.fori_loop(0, 16, first, 0)
    vb[2] = jnp.zeros((D, D), F32)
    bp[...] = jnp.zeros(TILE, F32)
    ab_ref[half] = jnp.zeros(TILE, F32)

    for o in own[:4]:
        o.wait()
    ei = lax.broadcasted_iota(jnp.int32, (D, 16), 0) // 16
    ej = lax.broadcasted_iota(jnp.int32, (D, 16), 1)
    spread = (ei == ej).astype(F32).astype(BF)
    fi = lax.broadcasted_iota(jnp.int32, (H, D), 0)
    fj = lax.broadcasted_iota(jnp.int32, (H, D), 1) // 16
    for k in range(KC):
        fk[k] = (fi == fj + 16 * k).astype(F32).astype(BF)

    def expand(d, carry):
        src = s ^ d
        when(d > 0, lambda: rcopy(w_ref, wb.at[src], wss.at[d], wsr.at[src], me ^ (2 * d)).wait_recv())
        mi = lax.broadcasted_iota(jnp.int32, (D, D), 0) & 15
        mj = lax.broadcasted_iota(jnp.int32, (D, D), 1) & 15
        x = jnp.dot(spread, wb[src], preferred_element_type=F32).astype(BF)
        for k in range(KC):
            e = jnp.dot(x, fk[k], preferred_element_type=F32)
            kr[src, k] = jnp.where(mi == mj, e, 0.0).astype(BF)
        return carry

    lax.fori_loop(0, 16, expand, 0)

    zend = jnp.logical_or(z == 0, z == 3)

    def line(g):
        near = jnp.where(zend, 2, 3)
        step = jnp.where(g == 0, 0, jnp.where(g == 1, 1, jnp.where(g == 2, near, 5 - near)))
        return s ^ (4 * step)

    def arrive(n):
        g, e = n // 4, lax.rem(n, 4)
        base = line(g)
        src = base ^ e

        @pl.when(jnp.logical_and(e == 0, g > 0))
        def _():
            zb = base // 4
            for h in range(2):
                wait_l(base, h)
            up = jnp.logical_and(zb < z, z < 3)
            down = jnp.logical_and(zb > z, z > 0)
            for h in range(2):
                when(up, z_copy(base, g, h, me + 8).start)
                when(down, z_copy(base, g, h, me - 8).start)
            for cp in xy_copies(base, g):
                cp.start()

        @pl.when(n == 4)
        def _():
            for d in range(8, 16):
                r_copy(d).start()

        @pl.when(e == 1)
        def _():
            wait_l(src, 0)
            f_copy(src, g, 0).start()
            wait_l(base ^ 2, 1)
            f_copy(base ^ 2, g, 1).start()
            wait_l(src, 1)

        when(e == 2, lambda: wait_l(src, 0))

        @pl.when(e == 3)
        def _():
            for h in range(2):
                wait_l(src, h)

        when(n > 0, lambda: rcopy(rb.at[src], rb.at[src], rss.at[1], rsr.at[src], xn).wait_recv())
        for k in range(KC):
            lb[src, k, 384:512, :] = lb[src, k, 0:H, :].T

    def right(s0, cnt, u0, y0):
        rr = rb[pl.ds(s0, cnt)].reshape(cnt * KC * 32, D)
        for du in range(4):
            yu = jnp.dot(rr, ub[u0 + du], preferred_element_type=F32).astype(BF).reshape(cnt, KC, 2, 16, D)
            at = pl.ds(pl.multiple_of(16 * (u0 + du), 16), 16)
            for t in range(2):
                y[pl.ds(y0, cnt), :, at, t * D:(t + 1) * D] = yu[:, :, t]

    def chunk(j, n):
        src = line(n // 4) ^ lax.rem(n, 4)
        slot = lax.rem(src, 8)
        when(j == 0, lambda: arrive(n))

        @pl.when(jnp.logical_or(j == 0, n >= 8))
        def _():
            for i in range(4):
                right(src, 1, 4 * i, slot)

        hk = KC // 2
        for h in range(2):
            for k in range(hk):
                zk = jnp.dot(kr[src, hk * h + k], y[slot, hk * h + k], preferred_element_type=F32).astype(BF)
                for t in range(2):
                    zz[t * D:(t + 1) * D, k * D:(k + 1) * D] = zk[:, t * D:(t + 1) * D]
            lk = lb.at[src, hk * h:hk * (h + 1)]
            rhs = jnp.concatenate([lk[:, D:512, :].reshape(hk * D, H), lk[:, 0:D, :].reshape(hk * D, H)], axis=1)
            acc[...] += jnp.dot(zz[...], rhs, preferred_element_type=F32).reshape(2, D, D)

    row = lax.broadcasted_iota(jnp.int32, TILE, 0)
    lane = lax.broadcasted_iota(jnp.int32, TILE, 1)

    def mine(src, g):
        return ub.at[pl.ds(4 * g, 4), pl.ds(pl.multiple_of(16 * src, 16), 16), :]

    def u_copy(d, g):
        return rcopy(mine(m, g), mine(m, g), uss.at[d, g], usr.at[m, g], 16 * half + (m ^ d))

    def u_fwd(d, g):
        return rcopy(mine(m ^ d, g), mine(m ^ d, g), ufs.at[d, g], usr.at[m ^ d, g], sib)

    def u_wait(src, g):
        rcopy(mine(src, g), mine(src, g), uss.at[1, 0], usr.at[src, g], sib).wait_recv()

    def sc_copy(d):
        return rcopy(sc_out, sc_in.at[m], sss.at[d], ssr.at[m], 16 * half + (m ^ d))

    def out_copy(j, p, k):
        return rcopy(tb.at[j, pl.ds(pl.multiple_of(8 * p, 8), 8), :], rx.at[j, me], oss.at[0], osr.at[k], p)

    def step(j, carry):
        @pl.when(j > 0)
        def _():
            def group(g, carry):
                for d in NEAR:
                    u_wait(m ^ d, g)
                    u_fwd(d, g).start()
                for d in range(1, 16, 2):
                    u_wait(m ^ d, g)

                for p in (0, 4):
                    right(8 * half + p, 4, 4 * g, p)
                for d in (1,) + NEAR:
                    u_copy(d, g).wait_send()
                for d in NEAR:
                    u_fwd(d, g).wait_send()
                return carry

            lax.fori_loop(0, 4, group, 0)

        acc[...] = jnp.zeros((2, D, D), F32)

        def chunks(n, carry):
            chunk(j, n)
            return carry

        lax.fori_loop(0, 16, chunks, 0)
        swap = rcopy(acc.at[1 - c], got, sw.at[0], sw.at[1], sib)
        swap.start()
        swap.wait()
        i0, i1, i2 = lax.rem(j, 3), lax.rem(j + 1, 3), lax.rem(j + 2, 3)
        v = vb[i0]
        w = acc[c] + got[...]
        w2 = w - bp[0:1, 0:1] * vb[i2]
        s1 = jnp.sum(w * v)
        s4 = jnp.sum(v * v)
        sh = jnp.sum(w2 * v) / jnp.where(s4 > 0, s4, 1.0)
        w3 = w2 - sh * v
        s2 = jnp.sum(w3 * w3)
        s3 = jnp.sum(w3 * v)
        tile = jnp.zeros(TILE, F32)
        for n, val in enumerate((s1, s2, s3, s4, sh)):
            tile = jnp.where(row == n, val, tile)
        sc_out[...] = tile
        sc_in[m] = tile
        for d in range(1, 16):
            sc_copy(d).start()
        for d in range(1, 16):
            rcopy(sc_out, sc_in.at[m ^ d], sss.at[d], ssr.at[m ^ d], sib).wait_recv()
        alpha = jnp.zeros((1, 1), F32)
        for d in range(16):
            alpha = alpha + sc_in[d, 0:1, 0:1]
        alpha = alpha / N_ELEMS
        beta2 = jnp.zeros((1, 1), F32)
        for d in range(16):
            dl = alpha - sc_in[d, 4:5, 0:1]
            beta2 = beta2 + (sc_in[d, 1:2, 0:1] - 2.0 * dl * sc_in[d, 2:3, 0:1] + dl * dl * sc_in[d, 3:4, 0:1])
        beta = jnp.sqrt(jnp.maximum(beta2, 0.0) / N_ELEMS)
        vn = (w2 - alpha * v) / beta
        more = j < STEPS - 1

        @pl.when(more)
        def _():
            ub[:, pl.ds(b0, 16), :] = vn.astype(BF).reshape(16, 16, D)

        vb[i1] = vn

        @pl.when(more)
        def _():
            for g in range(4):
                for d in (14, 6, 10, 12, 2, 4, 8, 1):
                    u_copy(d, g).start()

        bp[...] = jnp.broadcast_to(beta, TILE)
        ab = jnp.where(row == 0, jnp.broadcast_to(alpha, TILE), jnp.broadcast_to(beta, TILE))
        ab_ref[half] = jnp.where(lane == j, ab, ab_ref[half])
        tb[j] = vb[i1].T
        rx[j, me] = tb[j, pl.ds(pl.multiple_of(8 * me, 8), 8), :]
        k = jnp.where(more, 0, 1)

        @pl.when(jnp.logical_not(more))
        def _():
            for d in range(31, 0, -1):
                out_copy(j, me ^ d, 1).start()

        @pl.when(more)
        def _():
            for d in range(31, 0, -1):
                out_copy(j, me ^ d, 0).start()

        for d in range(1, 16):
            sc_copy(d).wait_send()
        return carry

    lax.fori_loop(0, STEPS, step, 0)

    cross = rcopy(ab_ref.at[half], ab_ref.at[half], cs.at[0], cs.at[1], me ^ 16)
    cross.start()
    ncp.wait()
    for r in range(2):
        v0b[r] = v0b[r] / jnp.where(half == r, norm, nt_in[0:1, 0:1].reshape(1, 1, 1, 1))
        pltpu.make_async_copy(v0b.at[r], o_ref.at[r, 0], osem.at[2 + r]).start()
    grp = lane // 16

    def regroup(n, carry):
        j = n // 2
        r = lax.rem(n, 2)
        when(j > 0, lambda: pltpu.make_async_copy(ost.at[r], o_ref.at[r, j], osem.at[r]).wait())
        for h in range(2):
            for hb in range(2):
                xv = [rx[j, 16 * r + 8 * hb + q, :, h * H:(h + 1) * H] for q in range(8)]
                for d in (1, 2, 4):
                    low = (grp & d) == 0
                    for a in range(8):
                        if a & d == 0:
                            p, q = xv[a], xv[a + d]
                            xv[a] = jnp.where(low, p, pltpu.roll(q, 16 * d, 1))
                            xv[a + d] = jnp.where(low, pltpu.roll(p, H - 16 * d, 1), q)
                for q in range(8):
                    ost[r, :, h * 2 + q // 4, q % 4, hb * H:(hb + 1) * H] = xv[q]
        pltpu.make_async_copy(ost.at[r], o_ref.at[r, j + 1], osem.at[r]).start()
        return carry

    def arrived(lo, cnt, k):
        ref = rx.at[pl.ds(lo, cnt), pl.ds(0, 31)]
        rcopy(ref, ref, oss.at[0], osr.at[k], sib).wait_recv()

    arrived(0, STEPS - 1, 0)
    lax.fori_loop(0, 2 * (STEPS - 1), regroup, 0)
    arrived(STEPS - 1, 1, 1)
    lax.fori_loop(2 * (STEPS - 1), 2 * STEPS, regroup, 0)
    for r in range(2):
        pltpu.make_async_copy(ost.at[r], o_ref.at[r, STEPS], osem.at[r]).wait()
        pltpu.make_async_copy(v0b.at[r], o_ref.at[r, 0], osem.at[2 + r]).wait()
    ref = rx.at[:, pl.ds(0, 31)]
    rcopy(ref, ref, oss.at[0], osr.at[0], sib).wait_send()
    cross.wait()
    for d in range(1, 16):
        w_copy(d).wait_send()
        r_copy(d).wait_send()
    for h in range(2):
        when(z < 3, z_copy(s, 0, h, me + 8, True).wait_send)
        when(z > 0, z_copy(s, 4, h, me - 8, True).wait_send)
    for cp in xy_copies(s, 0, True):
        cp.wait_send()
    for g in range(4):
        base = line(g)
        if g:
            zb = base // 4
            for h in range(2):
                when(jnp.logical_and(zb < z, z < 3), z_copy(base, g, h, me + 8).wait_send)
                when(jnp.logical_and(zb > z, z > 0), z_copy(base, g, h, me - 8).wait_send)
            for cp in xy_copies(base, g):
                cp.wait_send()
        f_copy(base ^ 1, g, 0).wait_send()
        f_copy(base ^ 2, g, 1).wait_send()


def lanczos(psi, l_loc, w_loc, r_loc):
    any_ = pl.BlockSpec(memory_space=pl.ANY)
    vm = pl.BlockSpec(memory_space=VM)
    dma = pltpu.SemaphoreType.DMA
    scratch = [
        VM((16, 8, 512, H), BF), VM((16, 8, D, D), BF), VM((16, 8, 32, D), BF), VM((16, 16, H), BF),
        VM((16, D, D), BF), VM((8, KC, D, 512), BF), VM((512, KC * H), BF), VM((2, D, D), F32), VM((D, D), F32),
        VM((3, D, D), F32), VM((4, D, D), F32), VM((2, 8, 4, 4, D), F32), VM((KC, H, D), BF),
        VM((STEPS, D, D), F32), VM((STEPS, 32, 8, D), F32), VM((2, 8, 4, 4, D), F32),
        VM(TILE, F32), VM((16, 8, H), F32), VM(TILE, F32), VM(TILE, F32), VM(TILE, F32),
        dma((4,)), dma((4,)), dma((4,)), dma((5, 2)), dma((4, 4)), dma((4, 2)), dma((16, 2)), dma((16,)), dma((16,)), dma((16,)), dma((16,)),
        dma((2,)), dma((2,)), dma((16,)), dma((16,)), dma((16, 4)), dma((16, 4)), dma((16, 4)), dma((1,)), dma((2,)), dma((2,)),
    ]
    return pl.pallas_call(
        lanczos_kernel,
        out_shape=(jax.ShapeDtypeStruct((2, STEPS + 1, 8, 4, 4, D), F32), jax.ShapeDtypeStruct((2, 8, H), F32)),
        in_specs=[any_] * 4,
        out_specs=(any_, vm),
        scratch_shapes=scratch,
        compiler_params=pltpu.CompilerParams(collective_id=0, has_side_effects=True, vmem_limit_bytes=63 * 2**20),
    )(psi, l_loc, w_loc, r_loc)


def solution(mesh):
    def device_fn(psi, l_loc, w_loc, r_loc):
        w = w_loc.transpose(2, 0, 1).reshape(16, H)
        l = jnp.concatenate([l_loc[:, :, H:], l_loc[:, :H, :H]], axis=1)
        vecs, ab = lanczos(psi, l, w, r_loc)
        return vecs, ab[:, 0, :STEPS], ab[:, 1, :STEPS]

    return jax.shard_map(device_fn, mesh=mesh, in_specs=(P(), P("terms"), P("terms"), P("terms")),
                         out_specs=(P(None, None, "terms"), P(), P()), check_vma=False)
```

time: 2320 us -> 460 us (0.20)
  waiting for transfers between devices: 1190 us -> 0 us
  matrix products: 524 us -> 0 us
  blocking collectives: 467 us -> 0 us
  Pallas kernels: 0 us -> 452 us
  local copies, waits for them, and re-layouts: 84.7 us -> 6.24 us
  other arithmetic: 29.3 us -> 0.93 us
    reduce_scatter x6 -> x0, waiting for transfers between devices: 880 us -> none  [device_fn(): lax.psum_scatter(part_sigma, 'terms', scatter_dimension=1, tiled=True)]
    dot_general x18 -> x0, matrix products: 524 us -> none  [the longest x6 198 us: device_fn(): jnp.einsum('kqu,krcub->krcqb', phys_loc, right_part, preferred_element_ty...]
    psum x12 -> x0, blocking collectives: 467 us -> none  [the longest x6 246 us: device_fn(): lax.psum(jnp.sum(residual * residual, axis=(1, 2, 3)), 'terms') / n_elems]
    pallas_call x0 -> x1, Pallas kernels: none -> 452 us  [lanczos(): pl.pallas_call(lanczos_kernel, out_shape=(jax.ShapeDtypeStruct((2, STEPS...]
    all_gather x5 -> x0, waiting for transfers between devices: 312 us -> none  [device_fn(): lax.all_gather(v_next.astype(jnp.bfloat16), 'terms', axis=1, tiled=True)]
    transpose x6 -> x0, local copies, waits for them, and re-layouts: 61.9 us -> none  [device_fn(): jnp.einsum('kac,krcqb->raqb', left_loc, mid_part, preferred_element_type=...]
  transfers between devices with their start and end apart: 11 -> 0, of which waited for: 11 -> 0; matrix products, arithmetic and copies ran while one was open for 0% -> 0% of each run, Pallas kernels for 0% -> 0%
where the time goes in v2:
time: 460 us
  Pallas kernels  452 us (98%)
  local copies, waits for them, and re-layouts  6.24 us (1%)
    pallas_call x1, Pallas kernels, lanczos(): pl.pallas_call(lanczos_kernel, out_shape=(jax.ShapeDtypeStruct((2, STEPS...  452 us

profile of v2, /device:TPU:0, one launch (start us, length us, event | category | flops | bytes accessed | tf_op | source)
XLA Modules:
  0.0 459.8 jit_solution(3496238573220157256)
XLA Ops:
  0.6 0.0 slice-start
  0.6 0.0 copy-start
  0.7 1.0 slice.13
  1.7 0.1 slice-done
  1.8 0.9 pad_maximum_fusion.l_ref
  2.7 0.0 copy-done
  2.7 0.7 copy.8.w_ref
  3.4 451.9 %shard_map.67 = (f32[2,7,8,4,4,256]{5,4,3,2,1,0:T(4,128)}, f32[2,8,128]{2,1,0:T(8,128)}) custom-call(f32[2,256,4,4,256]{4,3,2,1,0:T(4,128)} %psi.1, bf16[8,384,128]{2,1,0:T(8,128)(2,1)} %pad_maximum_fusion.l_ref, bf16[16,128]{1,0:T(8,128)(2,1)} %copy.8.w_ref, bf16[8,256,256]{2,1,0:T(8,128)(2,1)} %r_ref.1), custom_call_target="tpu_custom_call" | custom-call | tf_op jit(solution)/shard_map/pallas_call | solution.py:414
  455.3 1.3 fusion
  456.6 3.1 copy.10
Async XLA Ops:
  0.6 1.1 slice-start
  0.6 2.0 copy-start

commit v3 on v2

--- a/solution.py
+++ b/solution.py
@@ -88,7 +88,7 @@
     for h in range(2):
         when(z < 3, z_copy(s, 0, h, me + 8, True).start)
         when(z > 0, z_copy(s, 4, h, me - 8, True).start)
-    for d in range(1, 8):
+    for d in (1, 2, 3, 4, 8, 5, 6, 7) + tuple(range(9, 16)):
         r_copy(d).start()
     for cp in xy_copies(s, 0, True):
         cp.start()
@@ -167,11 +167,6 @@
             for cp in xy_copies(base, g):
                 cp.start()
 
-        @pl.when(n == 4)
-        def _():
-            for d in range(8, 16):
-                r_copy(d).start()
-
         @pl.when(e == 1)
         def _():
             wait_l(src, 0)
@@ -259,6 +254,8 @@
                 return carry
 
             lax.fori_loop(0, 4, group, 0)
+            for d in range(31, 0, -1):
+                out_copy(j - 1, me ^ d, 0).start()
 
         acc[...] = jnp.zeros((2, D, D), F32)
 
@@ -318,17 +315,11 @@
         ab_ref[half] = jnp.where(lane == j, ab, ab_ref[half])
         tb[j] = vb[i1].T
         rx[j, me] = tb[j, pl.ds(pl.multiple_of(8 * me, 8), 8), :]
-        k = jnp.where(more, 0, 1)
 
         @pl.when(jnp.logical_not(more))
         def _():
             for d in range(31, 0, -1):
                 out_copy(j, me ^ d, 1).start()
-
-        @pl.when(more)
-        def _():
-            for d in range(31, 0, -1):
-                out_copy(j, me ^ d, 0).start()
 
         for d in range(1, 16):
             sc_copy(d).wait_send()

time: 460 us -> 443 us (0.963)
  Pallas kernels: 452 us -> 434 us
    pallas_call x1, Pallas kernels: 452 us -> 434 us  [lanczos(): pl.pallas_call(lanczos_kernel, out_shape=(jax.ShapeDtypeStruct((2, STEPS...]
where the time goes in v3:
time: 443 us; the launch traced here: 442 us
  Pallas kernels  434 us (98%)
  local copies, waits for them, and re-layouts  6.24 us (1%)
    pallas_call x1, Pallas kernels, lanczos(): pl.pallas_call(lanczos_kernel, out_shape=(jax.ShapeDtypeStruct((2, STEPS...  434 us

profile of v3, /device:TPU:0, one launch (start us, length us, event | category | flops | bytes accessed | tf_op | source)
XLA Modules:
  0.0 442.2 jit_solution(18421050827547959978)
XLA Ops:
  0.6 0.0 slice-start
  0.6 0.0 copy-start
  0.7 1.0 slice.13
  1.7 0.1 slice-done
  1.8 0.9 pad_maximum_fusion.l_ref
  2.7 0.0 copy-done
  2.7 0.7 copy.8.w_ref
  3.4 434.4 %shard_map.67 = (f32[2,7,8,4,4,256]{5,4,3,2,1,0:T(4,128)}, f32[2,8,128]{2,1,0:T(8,128)}) custom-call(f32[2,256,4,4,256]{4,3,2,1,0:T(4,128)} %psi.1, bf16[8,384,128]{2,1,0:T(8,128)(2,1)} %pad_maximum_fusion.l_ref, bf16[16,128]{1,0:T(8,128)(2,1)} %copy.8.w_ref, bf16[8,256,256]{2,1,0:T(8,128)(2,1)} %r_ref.1), custom_call_target="tpu_custom_call" | custom-call | tf_op jit(solution)/shard_map/pallas_call | solution.py:405
  437.7 1.3 fusion
  439.1 3.1 copy.10
Async XLA Ops:
  0.6 1.1 slice-start
  0.6 2.0 copy-start
